TPU v7x, 32 devices: a whole 2x2x4 slice. The times are simulated.
32 devices in a mesh: grp: 2 (over y), ka: 4 (over z), orb: 2 (over x), band: 2 (over core).
Axes of the slice: x: 2, y: 2, z: 4, core: 2. Of those that a mesh axis runs over, the one named last changes fastest.
Arguments:
- eigvecs: bfloat16 [8, 2, 8192, 256], P(('grp', 'ka'), None, 'orb', 'band'), parts along dimension 0, may hold values from -0.03515625 to 0.03515625
- band_rank: int32 [8, 256], P(('grp', 'ka'), 'band'), parts along dimension 0, may hold values from 0 to 255, each once within a row
- occ_count: int32 [2], P('grp'), parts along dimension 0, may hold values from 128 to 256
- wrap_shift: int32 [2], P('grp'), parts along dimension 0, may hold values from 1 to 4095
- orbital_site: int32 [16384], P(('grp', 'orb')), parts along dimension 0, may hold values from 0 to 63
Outputs:
- wilson: float32 [8, 256, 2, 256], P(('grp', 'ka'), 'orb', None, 'band'), parts along dimension 0
There are 2 independent parts, one for each index of `grp`. A program takes and returns all parts, laid end to end along the dimension named above; each array names one. Nothing has to cross between parts.
All inputs are finite; a program needn't handle non-finite values.
Results may differ from a plain program's by a relative error of at most 0.025.
Values may be sent and summed in bfloat16 or wider, within the bound.
A program may use at most 64 MiB of HBM per device.

v0:
```python
import math

import jax
import jax.numpy as jnp
from jax import lax
from jax.sharding import PartitionSpec as P

NS_STEPS = 8
SITES = 64


ns_gain = 0.7
eps_mean = 1e-06


def from_behind(value, axis, by):
    count = lax.axis_size(axis)
    return lax.ppermute(value, axis, [(i, (i + by) % count) for i in range(count)])


def entering(value, axis, join, neutral):
    count, mine = (lax.axis_size(axis), lax.axis_index(axis))
    pieces = lax.all_gather(value, axis)
    subtotal = jnp.full_like(value, 0) + jnp.asarray(neutral, value.dtype)

    def lap(position, subtotal):
        longer = join(subtotal, pieces[position])
        return jnp.where(position < mine, longer, subtotal)

    return lax.fori_loop(0, count - 1, lap, subtotal)


def complex_block(matrix):
    order_size = matrix.shape[0]
    real_part = matrix[:, :order_size]
    imag_part = matrix[:, order_size:]
    upper_half = jnp.concatenate([real_part, imag_part], axis=1)
    lower_half = jnp.concatenate([-imag_part, real_part], axis=1)
    return jnp.concatenate([upper_half, lower_half], axis=0)


def complex_product(left_side, right_side):
    return jnp.dot(
        left_side,
        complex_block(right_side),
        precision=lax.Precision.HIGHEST,
        preferred_element_type=jnp.float32,
    )


def polar_step(iterate):
    order_size = iterate.shape[1]
    rounded = iterate.astype(jnp.bfloat16)
    gram_matrix = jnp.einsum("kri,krj->kij", rounded, rounded, preferred_element_type=jnp.float32)
    gram_real = gram_matrix[:, :order_size, :order_size] + gram_matrix[:, order_size:, order_size:]
    gram_imag = gram_matrix[:, :order_size, order_size:] - gram_matrix[:, order_size:, :order_size]
    upper_half = jnp.concatenate([gram_real, gram_imag], axis=2)
    lower_half = jnp.concatenate([-gram_imag, gram_real], axis=2)
    gram_block = jnp.concatenate([upper_half, lower_half], axis=1).astype(jnp.bfloat16)
    product = jnp.einsum("kri,kij->krj", rounded, gram_block, preferred_element_type=jnp.float32)
    return 1.5 * iterate - 0.5 * product


def turn_block(arrived, phase_angle, at_end):
    cosine = jnp.cos(phase_angle)[:, None]
    sine_factor = jnp.sin(phase_angle)[:, None]
    first_real = arrived[0].astype(jnp.float32)
    first_imag = arrived[1].astype(jnp.float32)
    turned = jnp.stack(
        [
            cosine * first_real + sine_factor * first_imag,
            cosine * first_imag - sine_factor * first_real,
        ]
    ).astype(jnp.bfloat16)
    return jnp.where(at_end, turned, arrived)


def margin_terms(lefts, rights):
    kpoints = lefts.shape[0]
    orbital_rows = lefts.shape[2]
    stacked = lefts.reshape(kpoints, 2 * orbital_rows, lefts.shape[3])
    real_side = rights.reshape(kpoints, 2 * orbital_rows, rights.shape[3])
    imag_side = jnp.concatenate([rights[:, 1], -rights[:, 0]], axis=1)
    paired = jnp.concatenate([real_side, imag_side], axis=2)
    return jnp.einsum("kor,koc->rkc", stacked, paired, preferred_element_type=jnp.float32)


def body(eigvecs, band_rank, occ_count, wrap_shift, orbital_site):
    kpoints = eigvecs.shape[0]
    band_cols = eigvecs.shape[3]
    band_total = band_cols * lax.axis_size("band")
    occupied = band_rank < occ_count[0]
    masked = jnp.where(occupied[:, None, None, :], eigvecs, jnp.zeros((), jnp.bfloat16))
    phase_angle = (wrap_shift[0] * orbital_site % SITES).astype(jnp.float32) * (
        2.0 * math.pi / SITES
    )
    at_end = lax.axis_index("ka") == lax.axis_size("ka") - 1
    arrived = from_behind(masked[0], "ka", -1)
    rights = jnp.concatenate([masked[1:], turn_block(arrived, phase_angle, at_end)[None]], axis=0)
    lefts = lax.all_gather(masked, "band", axis=3, tiled=True)
    reduced = lax.psum_scatter(margin_terms(lefts, rights), "orb", scatter_dimension=0, tiled=True)
    row_share = reduced.shape[0]
    gathered = lax.all_gather(
        reduced.reshape(1, row_share, kpoints, 2, band_cols), ("orb", "band"), axis=0, tiled=True
    )
    gathered = gathered.reshape(
        lax.axis_size("orb"), lax.axis_size("band"), row_share, kpoints, 2, band_cols
    )
    margins = gathered.transpose(3, 0, 2, 4, 1, 5).reshape(kpoints, band_total, 2 * band_total)
    occupied_total = occ_count[0].astype(jnp.float32)
    squares = jnp.sum(margins * margins, axis=(1, 2))
    iterate = margins * (ns_gain * lax.rsqrt(squares / occupied_total + eps_mean))[:, None, None]
    for sweep_index in range(NS_STEPS):
        iterate = polar_step(iterate)
    chain_local = iterate[0]
    identity = jnp.concatenate(
        [jnp.eye(band_total, dtype=jnp.float32), jnp.zeros((band_total, band_total), jnp.float32)],
        axis=1,
    )
    before = entering(chain_local, "ka", complex_product, identity)
    row_count = band_total // lax.axis_size("orb")
    running = lax.dynamic_slice_in_dim(before, lax.axis_index("orb") * row_count, row_count, 0)
    running = complex_product(running, iterate[0])
    shaped = running.reshape(row_count, 2, band_total)
    results = [lax.dynamic_slice_in_dim(shaped, lax.axis_index("band") * band_cols, band_cols, 2)]
    return jnp.stack(results) * math.sqrt(band_total)


def solution(mesh):
    return jax.shard_map(
        body,
        mesh=mesh,
        in_specs=(
            P(("grp", "ka"), None, "orb", "band"),
            P(("grp", "ka"), "band"),
            P("grp"),
            P("grp"),
            P(("grp", "orb")),
        ),
        out_specs=P(("grp", "ka"), "orb", None, "band"),
        check_vma=False,
    )
```

profile of v0, /device:TPU:0, one launch (start us, length us, event | category | flops | bytes accessed | tf_op | source)
XLA Modules:
  0.0 166.4 jit_solution(17715661902603029147)
XLA Ops:
  7.2 0.7 compare_bitcast_fusion
  7.9 3.3 %fusion.109 = bf16[2,4096,128]{2,1,0:T(8,128)(2,1)} fusion(bf16[1,2,4096,128]{3,2,1,0:T(8,128)(2,1)} %param.7, pred[128]{0:T(512)(128)(4,1)S(1)} %compare_bitcast_fusion), kind=kLoop, calls=%fused_computation.184 | loop fusion | flops 1048576 | bytes 4194432 | tf_op jit(solution)/shard_map/squeeze | solution.py:98
  11.1 5.1 %collective-permute-start = (bf16[2,4096,128]{2,1,0:T(8,128)(2,1)}, bf16[2,4096,128]{2,1,0:T(8,128)(2,1)S(1)}, u32[]{:S(2)}, u32[]{:S(2)}) collective-permute-start(bf16[2,4096,128]{2,1,0:T(8,128)(2,1)} %fusion.109), channel_id=1, source_target_pairs={{0,12},{4,0},{8,4},{12,8},{1,13},{5,1},{9,5},{13,9},{2,14},{6,2},{... | collective-permute-start | bytes 6291464 | tf_op jit(solution)/shard_map/ppermute | solution.py:18
  16.2 1.5 broadcast_select_fusion
  18.4 0.1 fusion.91
  18.5 42.9 %collective-permute-done = bf16[2,4096,128]{2,1,0:T(8,128)(2,1)S(1)} collective-permute-done((bf16[2,4096,128]{2,1,0:T(8,128)(2,1)}, bf16[2,4096,128]{2,1,0:T(8,128)(2,1)S(1)}, u32[]{:S(2)}, u32[]{:S(2)}) %collective-permute-start) | collective-permute-done | bytes 2097184 | tf_op jit(solution)/shard_map/ppermute | solution.py:18
  61.4 1.4 fusion.13
  62.8 0.3 fusion.108
  63.1 1.3 slice_bitcast_fusion
  64.3 1.7 %maximum_select_fusion = bf16[2,4096,128]{2,1,0:T(8,128)(2,1)} fusion(bf16[2,4096,128]{2,1,0:T(8,128)(2,1)S(1)} %collective-permute-done, bf16[1,4096,128]{2,1,0:T(8,128)(2,1)S(1)} %get-tuple-element.96, bf16[1,4096,128]{2,1,0:T(8,128)(2,1)S(1)} %get-tuple-element.95, pred[]{:T(512)S(6)} %eq.9), kind=kLoop, calls=%fused_computation.24 | loop fusion | flops 2097152 | bytes 6291457 | tf_op jit(solution)/shard_map/jit(_where)/select_n | solution.py:75
  66.0 5.1 %fusion.24 = f32[256,1,256]{0,2,1:T(8,128)} fusion(bf16[8192,256]{1,0:T(8,128)(2,1)} %bitcast.108, bf16[1,4096,128]{2,1,0:T(8,128)(2,1)} %get-tuple-element.98, bf16[1,4096,128]{2,1,0:T(8,128)(2,1)S(1)} %get-tuple-element.97, bf16[1,8192,128]{2,1,0:T(8,128)(2,1)} %bitcast.103), kind=kOutput, calls=%fused_computation.50 | convolution fusion | flops 1086324736 | bytes 8650752 | tf_op jit(solution)/shard_map/kor,koc->rkc/dot_general | solution.py:85
  71.2 13.7 %reduce-scatter.2.cloned.1.call-done = f32[128,1,256]{0,2,1:T(8,128)} async-done(((f32[256,1,256]{0,2,1:T(8,128)}), f32[128,1,256]{0,2,1:T(8,128)}) %reduce-scatter.2.cloned.1.call-update) | async-done | bytes 131088 | tf_op jit(solution)/shard_map/reduce_scatter | solution.py:101
  84.9 1.0 copy.11
  85.9 6.8 %all_gather.10 = f32[4,128,1,2,128]{4,1,3,2,0:T(8,128)S(1)} all-gather(f32[1,128,1,2,128]{4,1,3,2,0:T(8,128)S(1)} %copy.11), channel_id=1, replica_groups=mesh['grp'=2,'ka'=4,'orb'=2,'band'=2] {'orb','band'}, dimensions={0}, use_global_device_ids=true | all-gather | bytes 655360 | tf_op jit(solution)/shard_map/all_gather | solution.py:103
  92.7 0.7 multiply_reduce_fusion
  94.1 0.1 multiply_convert_fusion
  94.2 0.3 copy.13
  94.5 0.1 convert_element_type.106
  94.6 0.3 convolution_bitcast_fusion.8
  95.0 0.4 copy.15
  95.4 0.4 mul.181
  95.9 0.3 fusion.23
  96.2 0.3 convolution_bitcast_fusion.7
  96.7 0.3 fusion.22
  97.0 0.3 convolution_bitcast_fusion.6
  97.5 0.3 fusion.21
  97.9 0.3 convolution_bitcast_fusion.5
  98.3 0.3 fusion.20
  98.7 0.3 convolution_bitcast_fusion.4
  99.1 0.3 fusion.19
  99.5 0.3 convolution_bitcast_fusion.3
  100.0 0.3 fusion.18
  100.3 0.3 convolution_bitcast_fusion.2
  100.8 0.3 fusion.17
  101.1 0.3 convolution_bitcast_fusion.1
  101.6 1.2 fusion.16
  102.8 1.1 slice_negate_fusion.2
  103.9 45.2 %all-gather.6.cloned.1.call-done = f32[1024,512]{1,0:T(8,128)} async-done(((f32[256,512]{1,0:T(8,128)}), f32[1024,512]{1,0:T(8,128)}) %all-gather.6.cloned.1.call-update) | async-done | bytes 2097168 | tf_op jit(solution)/shard_map/all_gather | solution.py:23
  149.1 9.1 %while.13 = (s32[]{:T(128)}, f32[256,512]{0,1:T(8,128)S(1)}, s32[]{:T(128)}, f32[4,256,512]{2,1,0:T(8,128)}, s32[]{:T(128)}) while((s32[]{:T(128)}, f32[256,512]{0,1:T(8,128)S(1)}, s32[]{:T(128)}, f32[4,256,512]{2,1,0:T(8,128)}, s32[]{:T(128)}) %tuple.69), condition=%wide.region_3.4_spmd, body=%wide.region_2.3_spmd.sunk | while | flops 806027264 | bytes 5242955 | solution.py:30
  149.1 1.1 dynamic-slice_bitcast_fusion.2
  150.4 1.8 %fusion.115 = f32[256,512]{0,1:T(8,128)S(1)} fusion(f32[256,512]{0,1:T(8,128)S(1)} %copy.26, f32[256,256]{1,0:T(8,128)S(1)} %get-tuple-element.172, f32[256,256]{1,0:T(8,128)S(1)} %get-tuple-element.173, f32[256,512]{1,0:T(8,128)S(1)} %dynamic-slice_bitcast_fusion.2, pred[]{:T(512)S(6)} %lt.49), kind=kOutput, calls=%fused_computation.1.clone.1 | convolution fusion | flops 805961728 | bytes 2097153 | tf_op jit(solution)/shard_map/while/body/eval_jaxpr/dot_general | solution.py:43
  152.2 1.1 dynamic-slice_bitcast_fusion.2
  153.4 1.8 %fusion.115 = f32[256,512]{0,1:T(8,128)S(1)} fusion(f32[256,512]{0,1:T(8,128)S(1)} %copy.26, f32[256,256]{1,0:T(8,128)S(1)} %get-tuple-element.172, f32[256,256]{1,0:T(8,128)S(1)} %get-tuple-element.173, f32[256,512]{1,0:T(8,128)S(1)} %dynamic-slice_bitcast_fusion.2, pred[]{:T(512)S(6)} %lt.49), kind=kOutput, calls=%fused_computation.1.clone.1 | convolution fusion | flops 805961728 | bytes 2097153 | tf_op jit(solution)/shard_map/while/body/eval_jaxpr/dot_general | solution.py:43
  155.2 1.1 dynamic-slice_bitcast_fusion.2
  156.4 1.8 %fusion.115 = f32[256,512]{0,1:T(8,128)S(1)} fusion(f32[256,512]{0,1:T(8,128)S(1)} %copy.26, f32[256,256]{1,0:T(8,128)S(1)} %get-tuple-element.172, f32[256,256]{1,0:T(8,128)S(1)} %get-tuple-element.173, f32[256,512]{1,0:T(8,128)S(1)} %dynamic-slice_bitcast_fusion.2, pred[]{:T(512)S(6)} %lt.49), kind=kOutput, calls=%fused_computation.1.clone.1 | convolution fusion | flops 805961728 | bytes 2097153 | tf_op jit(solution)/shard_map/while/body/eval_jaxpr/dot_general | solution.py:43
  158.2 0.8 fusion.26
  159.0 0.2 reshape.299
  159.2 0.7 multiply_bitcast_fusion
  (37 shorter events, 1.3 us)
Async XLA Ops:
  6.5 59.5 %all-gather.4.cloned.1.call-start = ((), (), s32[]{:S(2)}) async-start(), calls=%async_computation.1 | async-start | bytes 6291456 | tf_op jit(solution)/shard_map/all_gather | solution.py:100
  7.9 8.4 %copy-start.1 = (bf16[1,2,4096,128]{3,2,1,0:T(8,128)(2,1)S(1)}, bf16[1,2,4096,128]{3,2,1,0:T(8,128)(2,1)}, u32[]{:S(2)}) copy-start(bf16[1,2,4096,128]{3,2,1,0:T(8,128)(2,1)} %param.7) | copy-start | bytes 6291460
  11.1 50.3 %collective-permute-start = (bf16[2,4096,128]{2,1,0:T(8,128)(2,1)}, bf16[2,4096,128]{2,1,0:T(8,128)(2,1)S(1)}, u32[]{:S(2)}, u32[]{:S(2)}) collective-permute-start(bf16[2,4096,128]{2,1,0:T(8,128)(2,1)} %fusion.109), channel_id=1, source_target_pairs={{0,12},{4,0},{8,4},{12,8},{1,13},{5,1},{9,5},{13,9},{2,14},{6,2},{... | collective-permute-start | bytes 6291464 | tf_op jit(solution)/shard_map/ppermute | solution.py:18
  17.7 0.7 copy-start.2
  17.7 67.1 %reduce-scatter.2.cloned.1.call-start = ((), (), s32[]{:S(2)}) async-start(), calls=%async_computation.2 | async-start | bytes 393216 | tf_op jit(solution)/shard_map/reduce_scatter | solution.py:101
  71.2 78.0 %all-gather.6.cloned.1.call-start = ((), (), s32[]{:S(2)}) async-start(), calls=%async_computation.3 | async-start | bytes 2621440 | tf_op jit(solution)/shard_map/all_gather | solution.py:23
  149.1 9.1 %copy-start = (f32[256,512]{1,0:T(8,128)S(1)}, f32[256,512]{1,0:T(8,128)}, u32[]{:S(2)}) copy-start(f32[256,512]{1,0:T(8,128)} %fusion.16) | copy-start | bytes 1572868
Sparse Core Ops, SparseCore 0:
  17.9 10.9 all-gather.3
  71.3 13.5 reduce-scatter.1
  102.9 46.2 all-gather.5
where the time goes:
time: 167 us; the launch traced here: 166 us
  waiting for transfers between devices  102 us (61%)
  matrix products  17.5 us (10%)
  between operations  15.4 us (9%)
  other arithmetic  13.8 us (8%)
  blocking collectives  6.8 us (4%)
  local copies, waits for them, and re-layouts  5.78 us (3%)
  starting transfers between devices  5.16 us (3%)
    all_gather x1, waiting for transfers between devices, entering(): pieces = lax.all_gather(value, axis)  45.2 us
    ppermute x1, waiting for transfers between devices, from_behind(): lax.ppermute(value, axis, [(i, (i + by) % count) for i in range(count)])  42.9 us
    reduce_scatter x1, waiting for transfers between devices, body(): lax.psum_scatter(margin_terms(lefts, rights), 'orb', scatter_dimension=0,...  13.7 us
    all_gather x1, blocking collectives, body(): lax.all_gather(reduced.reshape(1, row_share, kpoints, 2, band_cols), ('or...  6.8 us
    dot_general x4, matrix products, complex_product(): jnp.dot(left_side, complex_block(right_side), precision=lax.Precision.HIG...  6.2 us
    dot_general x1, matrix products, margin_terms(): jnp.einsum('kor,koc->rkc', stacked, paired, preferred_element_type=jnp.fl...  5.14 us
    ppermute x1, starting transfers between devices, from_behind(): lax.ppermute(value, axis, [(i, (i + by) % count) for i in range(count)])  5.08 us
    dot_general x8, matrix products, polar_step(): jnp.einsum('kri,kij->krj', rounded, gram_block, preferred_element_type=jn...  3.49 us
  transfers between devices with their start and end apart: 4, of which 3 were waited for; matrix products, arithmetic and copies ran while one was open for 4% of the time, Pallas kernels for 0%

commit v1 on v0

v1 whole, which is shorter than its diff:
```python
import functools
import math

import jax
import jax.numpy as jnp
from jax import lax
from jax.experimental import pallas as pl
from jax.experimental.pallas import tpu as pltpu
from jax.sharding import PartitionSpec as P

NS_STEPS = 8
SITES = 64
CHUNKS = 8

ns_gain = 0.7
eps_mean = 1e-06

MESH = pl.DeviceIdType.MESH
BF16 = jnp.bfloat16
F32 = jnp.float32


def levels_of(count):
    return max(1, (count - 1).bit_length())


def remote(src, dst, send_sem, recv_sem, device):
    return pltpu.make_async_remote_copy(
        src_ref=src,
        dst_ref=dst,
        send_sem=send_sem,
        recv_sem=recv_sem,
        device_id=device,
        device_id_type=MESH,
    )


def across(left, right, contract):
    return lax.dot_general(left, right, (contract, ((), ())), preferred_element_type=F32)


def column_of(row, width):
    return jnp.transpose(jnp.broadcast_to(row, (width, row.shape[1])))


def polar_step(iterate):
    half = iterate.shape[1] // 2
    rounded = iterate.astype(BF16)
    real, imag = rounded[:, :half], rounded[:, half:]
    tall = jnp.concatenate(
        [rounded, jnp.concatenate([imag, -real], axis=1)], axis=0
    )
    gram = across(tall, rounded, ((1,), (1,))).astype(BF16)
    rows = iterate.shape[0]
    wide = jnp.concatenate([gram[:rows], gram[rows:]], axis=1)
    block = jnp.concatenate(
        [rounded, jnp.concatenate([-imag, real], axis=1)], axis=0
    )
    product = across(wide, block, ((1,), (0,)))
    return 1.5 * iterate - 0.5 * product


def merge(pieces, factor):
    cols = factor.shape[1] // 2
    left = jnp.concatenate(
        [piece[:, :cols] for piece in pieces] + [piece[:, cols:] for piece in pieces], axis=1
    )
    lower = jnp.concatenate([-factor[:, cols:], factor[:, :cols]], axis=1)
    return across(left, jnp.concatenate([factor, lower], axis=0), ((1,), (0,)))


def kernel(
    nka, norb, nband,
    eig, rank, occ, shift, site,
    out,
    lefts, rights, cosine, sine, angle_cos, angle_sin,
    rank_band, rank_next, acc, part_out, part_in, whole, cur, pfx, got,
    sem_own, sem_left, sem_rank, sem_next, sem_right, sem_orb, sem_sum, sem_pre, sem_fwd,
):
    ka, orb, band = lax.axis_index("ka"), lax.axis_index("orb"), lax.axis_index("band")
    rows, cols = eig.shape[1], eig.shape[2]
    bands = nband * cols
    step = rows // CHUNKS
    before = lax.rem(ka + nka - 1, nka)

    barrier = pltpu.get_barrier_semaphore()
    greeted = 0
    for axis, mine, count in (("ka", ka, nka), ("band", band, nband), ("orb", orb, norb)):
        for d in range(1, count):
            pl.semaphore_signal(
                barrier, inc=1, device_id={axis: lax.rem(mine + d, count)}, device_id_type=MESH
            )
            greeted += 1
    pl.semaphore_wait(barrier, greeted)

    def chunk(c):
        return pl.ds(c * step, step)

    sends = []
    for c in range(CHUNKS):
        copy = remote(
            eig.at[:, chunk(c)], rights.at[:, chunk(c)],
            sem_right.at[0, c], sem_right.at[1, c], {"ka": before},
        )
        copy.start()
        sends.append(copy)
    next_rank = remote(rank, rank_next, sem_next.at[0], sem_next.at[1], {"ka": before})
    next_rank.start()
    own = pltpu.make_async_copy(eig, lefts.at[:, band], sem_own)
    own.start()
    band_sends = []
    for d in range(1, nband):
        to = {"band": lax.rem(band + d, nband)}
        copy = remote(eig, lefts.at[:, band], sem_left.at[0, d], sem_left.at[1, d], to)
        copy.start()
        band_sends.append(copy)
        copy = remote(rank, rank_band.at[band], sem_rank.at[0, d], sem_rank.at[1, d], to)
        copy.start()
        band_sends.append(copy)

    at_end = ka == nka - 1
    lanes = site.shape[1]
    angle = ((shift[0] * site[...]) & (SITES - 1)).astype(F32) * (2.0 * math.pi / SITES)
    angle_cos[...] = jnp.where(at_end, jnp.cos(angle), 1.0)
    angle_sin[...] = jnp.where(at_end, jnp.sin(angle), 0.0)

    @pl.loop(0, site.shape[0])
    def _(i):
        place = pl.ds(pl.multiple_of(i * lanes, lanes), lanes)
        cosine[place, :] = column_of(angle_cos[pl.ds(i, 1), :], cols)
        sine[place, :] = column_of(angle_sin[pl.ds(i, 1), :], cols)

    rank_band[band] = rank[...]
    own.wait()
    for d in range(1, nband):
        came = lax.rem(band + nband - d, nband)
        to = {"band": lax.rem(band + d, nband)}
        remote(eig, lefts.at[:, came], sem_left.at[0, d], sem_left.at[1, d], to).wait_recv()
        remote(rank, rank_band.at[came], sem_rank.at[0, d], sem_rank.at[1, d], to).wait_recv()
    next_rank.wait_recv()

    count = occ[0]
    row_mask = jnp.concatenate(
        [column_of((rank_band[j] < count).astype(F32), cols) for j in range(nband)], axis=0
    )
    row_mask = jnp.concatenate([row_mask, row_mask], axis=1)
    col_mask = (rank_next[...] < count).astype(F32)
    col_mask = jnp.concatenate([col_mask, col_mask], axis=1)
    mask = row_mask * col_mask > 0.5

    for c in range(CHUNKS):
        sends[c].wait_recv()
        real, imag = rights[0, chunk(c), :].astype(F32), rights[1, chunk(c), :].astype(F32)
        turn, lift = cosine[chunk(c), :], sine[chunk(c), :]
        new_real = (turn * real + lift * imag).astype(BF16)
        new_imag = (turn * imag - lift * real).astype(BF16)
        paired = jnp.concatenate(
            [
                jnp.concatenate([new_real, new_imag], axis=1),
                jnp.concatenate([new_imag, -new_real], axis=1),
            ],
            axis=0,
        )
        stacked = jnp.concatenate(
            [
                jnp.concatenate([lefts[p, j, chunk(c), :] for j in range(nband)], axis=1)
                for p in range(2)
            ],
            axis=0,
        )
        term = across(stacked, paired, ((0,), (0,)))
        if c == 0:
            acc[...] = term
        elif c < CHUNKS - 1:
            acc[...] += term
        else:
            part_out[...] = jnp.where(mask, acc[...] + term, 0.0).astype(BF16)

    part_sends = []
    for d in range(1, norb):
        copy = remote(
            part_out, part_in.at[d], sem_orb.at[0, d], sem_orb.at[1, d],
            {"orb": lax.rem(orb + d, norb)},
        )
        copy.start()
        part_sends.append(copy)
    total = part_out[...].astype(F32)
    for d in range(1, norb):
        part_sends[d - 1].wait_recv()
        total += part_in[d].astype(F32)
    whole[band] = total

    sum_sends = []
    for d in range(1, nband):
        copy = remote(
            whole.at[band], whole.at[band], sem_sum.at[0, d], sem_sum.at[1, d],
            {"band": lax.rem(band + d, nband)},
        )
        copy.start()
        sum_sends.append(copy)
    for d in range(1, nband):
        came = lax.rem(band + nband - d, nband)
        remote(
            whole.at[came], whole.at[came], sem_sum.at[0, d], sem_sum.at[1, d],
            {"band": lax.rem(band + d, nband)},
        ).wait_recv()
    margins = jnp.concatenate(
        [whole[j][:, :cols] for j in range(nband)] + [whole[j][:, cols:] for j in range(nband)],
        axis=1,
    )
    squares = jnp.sum(margins * margins, keepdims=True)
    iterate = margins * (ns_gain * lax.rsqrt(squares / count.astype(F32) + eps_mean))
    for _ in range(NS_STEPS):
        iterate = polar_step(iterate)

    def columns(j):
        at = [iterate[:, p * bands + j * cols : p * bands + (j + 1) * cols] for p in range(2)]
        return jnp.concatenate(at, axis=1)

    mine = columns(0)
    for j in range(1, nband):
        mine = jnp.where(band == j, columns(j), mine)
    cur[...] = mine.astype(BF16)
    share = bands // norb
    my_rows = pl.ds(pl.multiple_of(orb * share, share), share)
    scale = math.sqrt(bands)

    @pl.when(ka == 0)
    def _():
        acc[...] = mine
        out[...] = acc[my_rows, :] * scale
        pfx[...] = cur[my_rows, :]

    for level in range(levels_of(nka) if nka > 1 else 0):
        half = 1 << level
        first = ka < 2 * half
        for is_first in (True, False):
            if not is_first and 2 * half >= nka:
                continue
            height = share if is_first else bands
            source = pfx if is_first else cur
            here = first if is_first else jnp.logical_not(first)
            sending = jnp.logical_and(here, lax.rem(ka, 2 * half) == half - 1)
            taking = jnp.logical_and(here, lax.rem(ka // half, 2) == 1)

            def push(t, level=level, height=height, source=source):
                return remote(
                    source, got.at[level, band, pl.ds(0, height)],
                    sem_pre.at[0, level, t], sem_pre.at[1, level, 0],
                    {"ka": lax.rem(ka + t, nka)},
                )

            def pass_on(d, level=level, height=height):
                block = got.at[level, band, pl.ds(0, height)]
                return remote(
                    block, block, sem_fwd.at[0, level, d], sem_fwd.at[1, level, d],
                    {"band": lax.rem(band + d, nband)},
                )

            for t in range(half, 0, -1):
                @pl.when(jnp.logical_and(sending, ka + t < nka))
                def _(t=t, push=push):
                    push(t).start()

            for t in range(half, 0, -1):
                @pl.when(jnp.logical_and(sending, ka + t < nka))
                def _(t=t, push=push):
                    push(t).wait_send()

            @pl.when(taking)
            def _(level=level, height=height, is_first=is_first, push=push, pass_on=pass_on):
                push(1).wait_recv()
                for d in range(1, nband):
                    pass_on(d).start()
                for d in range(1, nband):
                    came = lax.rem(band + nband - d, nband)
                    block = got.at[level, came, pl.ds(0, height)]
                    remote(
                        block, block, sem_fwd.at[0, level, d], sem_fwd.at[1, level, d],
                        {"band": lax.rem(band + d, nband)},
                    ).wait_recv()
                pieces = [got[level, j, :height, :] for j in range(nband)]
                joined = merge(pieces, cur[...])
                if is_first:
                    out[...] = joined * scale
                    pfx[...] = joined.astype(BF16)
                else:
                    cur[...] = joined.astype(BF16)
                for d in range(1, nband):
                    pass_on(d).wait_send()

    for copy in sends + band_sends + part_sends + sum_sends + [next_rank]:
        copy.wait_send()


def solution(mesh):
    nka, norb, nband = mesh.shape["ka"], mesh.shape["orb"], mesh.shape["band"]
    depth = levels_of(nka)

    def body(eigvecs, band_rank, occ_count, wrap_shift, orbital_site):
        rows, cols = eigvecs.shape[2], eigvecs.shape[3]
        bands = cols * nband
        share = bands // norb
        vmem = pl.BlockSpec(memory_space=pltpu.VMEM)
        smem = pl.BlockSpec(memory_space=pltpu.SMEM)
        dma = pltpu.SemaphoreType.DMA
        result = pl.pallas_call(
            functools.partial(kernel, nka, norb, nband),
            out_shape=jax.ShapeDtypeStruct((share, 2 * cols), F32),
            in_specs=[pl.BlockSpec(memory_space=pl.ANY), vmem, smem, smem, vmem],
            out_specs=vmem,
            scratch_shapes=[
                pltpu.VMEM((2, nband, rows, cols), BF16),
                pltpu.VMEM((2, rows, cols), BF16),
                pltpu.VMEM((rows, cols), F32),
                pltpu.VMEM((rows, cols), F32),
                pltpu.VMEM((rows // 128, 128), F32),
                pltpu.VMEM((rows // 128, 128), F32),
                pltpu.VMEM((nband, 1, cols), jnp.int32),
                pltpu.VMEM((1, cols), jnp.int32),
                pltpu.VMEM((bands, 2 * cols), F32),
                pltpu.VMEM((bands, 2 * cols), BF16),
                pltpu.VMEM((norb, bands, 2 * cols), BF16),
                pltpu.VMEM((nband, bands, 2 * cols), F32),
                pltpu.VMEM((bands, 2 * cols), BF16),
                pltpu.VMEM((share, 2 * cols), BF16),
                pltpu.VMEM((depth, nband, bands, 2 * cols), BF16),
                dma,
                dma((2, nband)),
                dma((2, nband)),
                dma((2,)),
                dma((2, CHUNKS)),
                dma((2, norb)),
                dma((2, nband)),
                dma((2, depth, max(2, 1 << (depth - 1)) + 1)),
                dma((2, depth, nband)),
            ],
            compiler_params=pltpu.CompilerParams(
                collective_id=0, has_side_effects=True, vmem_limit_bytes=48 * 1024 * 1024
            ),
            name="wilson",
        )(
            eigvecs.reshape(2, rows, cols), band_rank, occ_count, wrap_shift,
            orbital_site.reshape(rows // 128, 128),
        )
        return result.reshape(1, share, 2, cols)

    return jax.shard_map(
        body,
        mesh=mesh,
        in_specs=(
            P(("grp", "ka"), None, "orb", "band"),
            P(("grp", "ka"), "band"),
            P("grp"),
            P("grp"),
            P(("grp", "orb")),
        ),
        out_specs=P(("grp", "ka"), "orb", None, "band"),
        check_vma=False,
    )
```

time: 167 us -> 77.3 us (0.46)
  the two profiles are of different devices: /device:TPU:0 before, /device:TPU:21 now
where the time goes in v1:
time: 77.3 us; the launch traced here: 77.1 us
  Pallas kernels  72.1 us (93%)
  local copies, waits for them, and re-layouts  3.68 us (5%)
  between operations  1.32 us (2%)
    pallas_call x1, Pallas kernels, body(): pl.pallas_call(functools.partial(kernel, nka, norb, nband), out_shape=jax...  72.1 us
    unnamed x6, local copies, waits for them, and re-layouts  2.96 us

profile of v1, /device:TPU:21, one launch (start us, length us, event | category | flops | bytes accessed | tf_op | source)
XLA Modules:
  0.0 77.1 jit_solution(4964640493683084571)
XLA Ops:
  1.3 0.0 copy-start
  1.3 1.6 %copy-done = bf16[1,2,4096,128]{3,2,1,0:T(8,128)(2,1)S(1)} copy-done((bf16[1,2,4096,128]{3,2,1,0:T(8,128)(2,1)S(1)}, bf16[1,2,4096,128]{3,2,1,0:T(8,128)(2,1)}, u32[]{:S(2)}) %copy-start) | copy-done | bytes 2097176
  2.9 0.0 copy-start.1
  2.9 0.7 copy-done.1
  3.6 0.0 copy-start.2
  3.6 0.7 copy-done.2
  4.3 72.1 %wilson.1 = f32[128,256]{1,0:T(8,128)S(1)} custom-call(bf16[2,4096,128]{2,1,0:T(8,128)(2,1)S(1)} %bitcast.2, s32[1,128]{1,0:T(1,128)S(1)} %copy-done.2, s32[1]{0:T(128)S(6)} %copy.6.occ, s32[1]{0:T(128)S(6)} %copy.7.shift, s32[32,128]{1,0:T(8,128)S(1)} %bitcast.3), custom_call_target="tpu_custom_call" | custom-call | tf_op jit(solution)/shard_map/wilson/pallas_call | solution.py:307
  76.4 0.7 reshape.11
Async XLA Ops:
  1.3 1.6 %copy-start = (bf16[1,2,4096,128]{3,2,1,0:T(8,128)(2,1)S(1)}, bf16[1,2,4096,128]{3,2,1,0:T(8,128)(2,1)}, u32[]{:S(2)}) copy-start(bf16[1,2,4096,128]{3,2,1,0:T(8,128)(2,1)} %param.5) | copy-start | bytes 6291460
  2.9 0.7 copy-start.1
  3.6 0.7 copy-start.2

commit v2 on v1

--- a/solution.py
+++ b/solution.py
@@ -10,7 +10,7 @@
 
 NS_STEPS = 8
 SITES = 64
-CHUNKS = 8
+CHUNKS = 16
 
 ns_gain = 0.7
 eps_mean = 1e-06
@@ -71,11 +71,11 @@
 
 def kernel(
     nka, norb, nband,
-    eig, rank, occ, shift, site,
+    eig, rank, occ_at, shift_at, site_at,
     out,
     lefts, rights, cosine, sine, angle_cos, angle_sin,
-    rank_band, rank_next, acc, part_out, part_in, whole, cur, pfx, got,
-    sem_own, sem_left, sem_rank, sem_next, sem_right, sem_orb, sem_sum, sem_pre, sem_fwd,
+    occ, shift, site, rank_band, rank_next, acc, part_out, part_in, whole, cur, pfx, got,
+    sem_own, sem_arg, sem_left, sem_rank, sem_next, sem_right, sem_orb, sem_sum, sem_pre, sem_fwd,
 ):
     ka, orb, band = lax.axis_index("ka"), lax.axis_index("orb"), lax.axis_index("band")
     rows, cols = eig.shape[1], eig.shape[2]
@@ -96,6 +96,8 @@
     def chunk(c):
         return pl.ds(c * step, step)
 
+    next_rank = remote(rank, rank_next, sem_next.at[0], sem_next.at[1], {"ka": before})
+    next_rank.start()
     sends = []
     for c in range(CHUNKS):
         copy = remote(
@@ -104,8 +106,14 @@
         )
         copy.start()
         sends.append(copy)
-    next_rank = remote(rank, rank_next, sem_next.at[0], sem_next.at[1], {"ka": before})
-    next_rank.start()
+    arguments = [
+        pltpu.make_async_copy(src, dst, sem_arg.at[i])
+        for i, (src, dst) in enumerate(
+            ((occ_at, occ), (shift_at, shift), (site_at, site), (rank, rank_band.at[band]))
+        )
+    ]
+    for copy in arguments:
+        copy.start()
     own = pltpu.make_async_copy(eig, lefts.at[:, band], sem_own)
     own.start()
     band_sends = []
@@ -118,6 +126,9 @@
         copy.start()
         band_sends.append(copy)
 
+    for copy in arguments:
+        copy.wait()
+
     at_end = ka == nka - 1
     lanes = site.shape[1]
     angle = ((shift[0] * site[...]) & (SITES - 1)).astype(F32) * (2.0 * math.pi / SITES)
@@ -130,7 +141,6 @@
         cosine[place, :] = column_of(angle_cos[pl.ds(i, 1), :], cols)
         sine[place, :] = column_of(angle_sin[pl.ds(i, 1), :], cols)
 
-    rank_band[band] = rank[...]
     own.wait()
     for d in range(1, nband):
         came = lax.rem(band + nband - d, nband)
@@ -301,14 +311,13 @@
         rows, cols = eigvecs.shape[2], eigvecs.shape[3]
         bands = cols * nband
         share = bands // norb
-        vmem = pl.BlockSpec(memory_space=pltpu.VMEM)
-        smem = pl.BlockSpec(memory_space=pltpu.SMEM)
+        hbm = pl.BlockSpec(memory_space=pltpu.HBM)
         dma = pltpu.SemaphoreType.DMA
         result = pl.pallas_call(
             functools.partial(kernel, nka, norb, nband),
             out_shape=jax.ShapeDtypeStruct((share, 2 * cols), F32),
-            in_specs=[pl.BlockSpec(memory_space=pl.ANY), vmem, smem, smem, vmem],
-            out_specs=vmem,
+            in_specs=[hbm] * 5,
+            out_specs=pl.BlockSpec(memory_space=pltpu.VMEM),
             scratch_shapes=[
                 pltpu.VMEM((2, nband, rows, cols), BF16),
                 pltpu.VMEM((2, rows, cols), BF16),
@@ -316,6 +325,9 @@
                 pltpu.VMEM((rows, cols), F32),
                 pltpu.VMEM((rows // 128, 128), F32),
                 pltpu.VMEM((rows // 128, 128), F32),
+                pltpu.SMEM((1,), jnp.int32),
+                pltpu.SMEM((1,), jnp.int32),
+                pltpu.VMEM((rows // 128, 128), jnp.int32),
                 pltpu.VMEM((nband, 1, cols), jnp.int32),
                 pltpu.VMEM((1, cols), jnp.int32),
                 pltpu.VMEM((bands, 2 * cols), F32),
@@ -326,6 +338,7 @@
                 pltpu.VMEM((share, 2 * cols), BF16),
                 pltpu.VMEM((depth, nband, bands, 2 * cols), BF16),
                 dma,
+                dma((4,)),
                 dma((2, nband)),
                 dma((2, nband)),
                 dma((2,)),
@@ -336,7 +349,7 @@
                 dma((2, depth, nband)),
             ],
             compiler_params=pltpu.CompilerParams(
-                collective_id=0, has_side_effects=True, vmem_limit_bytes=48 * 1024 * 1024
+                collective_id=0, has_side_effects=True, vmem_limit_bytes=67043328
             ),
             name="wilson",
         )(

time: 77.3 us -> 73.8 us (0.955)
  local copies, waits for them, and re-layouts: 3.68 us -> 1.62 us
  Pallas kernels: 72.1 us -> 70.6 us
    unnamed x6 -> x0, local copies, waits for them, and re-layouts: 2.96 us -> none
    pallas_call x1, Pallas kernels: 72.1 us -> 70.6 us  [body(): pl.pallas_call(functools.partial(kernel, nka, norb, nband), out_shape=jax...]
    reshape x1, local copies, waits for them, and re-layouts: 0.72 us -> 1.62 us  [body(): return result.reshape(1, share, 2, cols)]
where the time goes in v2:
time: 73.8 us; the launch traced here: 73.5 us
  Pallas kernels  70.6 us (96%)
  local copies, waits for them, and re-layouts  1.62 us (2%)
  between operations  1.3 us (2%)
    pallas_call x1, Pallas kernels, body(): pl.pallas_call(functools.partial(kernel, nka, norb, nband), out_shape=jax...  70.6 us
    reshape x1, local copies, waits for them, and re-layouts, body(): return result.reshape(1, share, 2, cols)  1.62 us

profile of v2, /device:TPU:21, one launch (start us, length us, event | category | flops | bytes accessed | tf_op | source)
XLA Modules:
  0.0 73.5 jit_solution(13457465145242951464)
XLA Ops:
  1.3 70.6 %wilson.1 = f32[128,256]{1,0:T(8,128)} custom-call(bf16[2,4096,128]{2,1,0:T(8,128)(2,1)} %bitcast.2, s32[1,128]{1,0:T(1,128)} %rank.1, s32[1]{0:T(128)S(6)} %copy.6.occ_at, s32[1]{0:T(128)S(6)} %copy.7.shift_at, s32[32,128]{1,0:T(8,128)} %bitcast.3), custom_call_target="tpu_custom_call" | custom-call | tf_op jit(solution)/shard_map/wilson/pallas_call | solution.py:316
  71.9 1.6 %reshape.11 = f32[1,128,2,128]{3,2,1,0:T(2,128)} reshape(f32[128,256]{1,0:T(8,128)} %wilson.1) | data formatting | bytes 262144 | tf_op jit(solution)/shard_map/reshape | solution.py:359
